TPU v7x, 512 devices: a whole 4x4x16 slice. The times are simulated.
512 devices in a mesh: cells: 32 (over x, y, core), vocab: 16 (over z).
Axes of the slice: x: 4, y: 4, z: 16, core: 2. Of those that a mesh axis runs over, the one named last changes fastest.
Arguments:
- clean_resid: float32 [32, 2048], P('cells'), may hold values from -130 to 130
- path_delta: bfloat16 [32, 4, 16, 2048], P('cells'), may hold values from -6 to 6
- layer_index: int32 [4064], P('cells'), may hold values from 0 to 3
- pos_index: int32 [4064], P('cells'), may hold values from 0 to 15
- answer_ids: int32 [32], P('cells'), may hold values from 0 to 51199
- norm_gain: float32 [2048], replicated, may hold values from 0.1 to 1.9
- unembed: bfloat16 [2048, 51200], P('cells', 'vocab'), may hold values from -1.5 to 1.5
Outputs:
- divergence: float32 [4064], P('cells')
- answer_logprob: float32 [4064], P('cells')
- total_kl: float32 [], replicated
All inputs are finite; a program needn't handle non-finite values.
Results may differ from a plain program's by a relative error of at most 0.0091.
Values may be sent and summed in bfloat16 or wider, within the bound.
No kernel may reach another device: no remote copies, remote signals or barrier semaphores. Data moves between devices by JAX's collectives and lax.ppermute only.
A program may use at most 64 MiB of HBM per device.

v0:
```python
import jax
import jax.numpy as jnp
from jax import lax
from jax.sharding import PartitionSpec as P


def sent_to_all(value, axis):
    length = lax.axis_size(axis)
    return lax.all_to_all(
        jnp.broadcast_to(value[None], (length, *value.shape)), axis, 0, 0, tiled=True
    )


def collected_together(value, axis):
    leaves = jax.tree.leaves(value)
    sequence = sorted(range(len(leaves)), key=lambda k: -leaves[k].size)
    width = (1, *leaves[sequence[0]].shape)[-1]
    lines = [
        jnp.pad(leaves[k].reshape(-1), (0, -leaves[k].size % width)).reshape(-1, width)
        for k in sequence
    ]
    both, at, found = (sent_to_all(jnp.concatenate(lines), axis), 0, {})
    for k, line in zip(sequence, lines):
        slab = both[:, at : at + len(line)].reshape(len(both), -1)
        found[k] = slab[:, : leaves[k].size].reshape(-1, *leaves[k].shape)
        at += len(line)
    numbers = iter(range(len(leaves)))
    return jax.tree.map(lambda _: found[next(numbers)], value)


def folded_in_pairs(pieces, combine):
    while len(jax.tree.leaves(pieces)[0]) > 1:
        pieces = jax.vmap(combine)(
            *(jax.tree.map(lambda part: part[side::2], pieces) for side in (0, 1))
        )
    return jax.tree.map(lambda part: part[0], pieces)


def merged_2(value, axis, combine):
    pieces = collected_together(value, axis)
    return folded_in_pairs(pieces, combine)


def of_everyone(value, axis):
    everything = sent_to_all(value, axis)
    return jnp.sum(everything, axis=0)


def normalize_rows(values, norm_gain):
    mean_square = jnp.mean(values * values, axis=-1, keepdims=True)
    return (values * lax.rsqrt(mean_square + 1e-06) * norm_gain).astype(jnp.bfloat16)


def local_partials(clean_logits, patched_logits, answer_mask, max_clean, max_patch):
    clean_exp = jnp.exp(clean_logits - max_clean[:, None])
    sum_clean = jnp.sum(clean_exp, axis=-1)
    cross_term = jnp.sum(
        clean_exp[:, None, :] * (clean_logits[:, None, :] - patched_logits), axis=-1
    )
    sum_patch = jnp.sum(jnp.exp(patched_logits - max_patch[..., None]), axis=-1)
    answer_sum = jnp.sum(jnp.where(answer_mask[:, None, :], patched_logits, 0.0), axis=-1)
    return (sum_clean, cross_term, sum_patch, answer_sum)


def combine_stats(earlier, later):
    max_one, sum_one, cross_one, patch_one, spat_one, answer_one = earlier
    max_two, sum_two, cross_two, patch_two, spat_two, answer_two = later
    max_clean = jnp.maximum(max_one, max_two)
    factor_one = jnp.exp(max_one - max_clean)
    factor_two = jnp.exp(max_two - max_clean)
    max_patch = jnp.maximum(patch_one, patch_two)
    pfactor_one = jnp.exp(patch_one - max_patch)
    pfactor_two = jnp.exp(patch_two - max_patch)
    return (
        max_clean,
        sum_one * factor_one + sum_two * factor_two,
        cross_one * factor_one[:, None] + cross_two * factor_two[:, None],
        max_patch,
        spat_one * pfactor_one + spat_two * pfactor_two,
        answer_one + answer_two,
    )


def finish_stats(max_clean, sum_clean, cross_term, max_patch, sum_patch, answer_sum):
    clean_lse = max_clean + jnp.log(sum_clean)
    patched_lse = max_patch + jnp.log(sum_patch)
    divergence = cross_term / sum_clean[:, None] - clean_lse[:, None] + patched_lse
    return (divergence, answer_sum - patched_lse)


def reduce_vocab(clean_logits, patched_logits, answer_mask):
    max_clean = jnp.max(clean_logits, axis=-1)
    max_patch = jnp.max(patched_logits, axis=-1)
    sum_clean, cross_term, sum_patch, answer_sum = local_partials(
        clean_logits, patched_logits, answer_mask, max_clean, max_patch
    )
    merged = merged_2(
        (max_clean, sum_clean, cross_term, max_patch, sum_patch, answer_sum), "vocab", combine_stats
    )
    return finish_stats(*merged)


def on_device(clean_resid, path_delta, layer_index, pos_index, answer_ids, norm_gain, unembed):
    position_count = path_delta.shape[2]
    table_rows = path_delta.shape[1] * position_count
    feature_count = clean_resid.shape[1]
    flat_index = layer_index * position_count + pos_index
    shard_width = unembed.shape[1]
    vocab_start = lax.axis_index("vocab") * shard_width
    delta_table = path_delta.reshape(table_rows, feature_count)
    picker = (flat_index[:, None] == jnp.arange(table_rows, dtype=jnp.int32)[None, :]).astype(
        jnp.bfloat16
    )
    patched_resid = clean_resid + jnp.dot(picker, delta_table, preferred_element_type=jnp.float32)
    stacked = jnp.concatenate(
        [normalize_rows(clean_resid, norm_gain), normalize_rows(patched_resid, norm_gain)], axis=0
    )
    logits = jnp.dot(
        stacked,
        lax.all_gather(unembed, "cells", axis=0, tiled=True),
        preferred_element_type=jnp.float32,
    )
    columns = vocab_start + jnp.arange(shard_width, dtype=jnp.int32)
    answer_mask = columns[None, :] == answer_ids[:, None]
    divergence, answer_logprob = reduce_vocab(logits[:1], logits[1:][None], answer_mask)
    divergence = divergence[0]
    answer_logprob = answer_logprob[0]
    total_kl = of_everyone(jnp.sum(divergence), "cells")
    return (divergence, answer_logprob, total_kl)


def solution(mesh):
    in_specs = (
        P("cells", None),
        P("cells", None, None, None),
        P("cells"),
        P("cells"),
        P("cells"),
        P(),
        P("cells", "vocab"),
    )
    out_specs = (P("cells"), P("cells"), P())
    return jax.shard_map(
        on_device, mesh=mesh, in_specs=in_specs, out_specs=out_specs, check_vma=False
    )
```

profile of v0, /device:TPU:1, one launch (start us, length us, event | category | flops | bytes accessed | tf_op | source)
XLA Modules:
  0.0 160.9 jit_solution(15475572089582252857)
XLA Ops:
  7.2 0.7 all-gather.2.cloned.1.call-update
  7.9 1.3 multiply_reduce_fusion.2
  10.6 0.7 multiply_add_fusion.9
  11.3 1.1 multiply_reduce_fusion.1
  12.5 0.2 multiply_convert_fusion
  12.7 83.6 %all-gather.2.cloned.1.call-done = bf16[2048,3200]{1,0:T(8,128)(2,1)} async-done(((bf16[64,3200]{1,0:T(8,128)(2,1)}), bf16[2048,3200]{1,0:T(8,128)(2,1)}) %all-gather.2.cloned.1.call-update) | async-done | bytes 13107216 | tf_op jit(solution)/shard_map/all_gather | solution.py:120
  96.2 6.7 %fusion = f32[128,3200]{1,0:T(8,128)S(1)} fusion(bf16[2048,3200]{1,0:T(8,128)(2,1)} %all-gather.2.cloned.1.call-done, bf16[127,2048]{1,0:T(8,128)(2,1)S(1)} %multiply_convert_fusion, bf16[1,2048]{1,0:T(2,128)(2,1)S(1)} %multiply_convert_fusion.1), kind=kOutput, calls=%fused_computation.7 | convolution fusion | flops 1678770176 | bytes 15269888 | tf_op jit(solution)/shard_map/dot_general | solution.py:118
  102.9 0.6 slice_reduce_fusion.2
  103.6 1.3 fusion.17
  104.9 0.6 select_reduce_fusion
  105.5 0.5 exponential_reduce_fusion
  105.9 1.3 pad_bitcast_fusion
  107.3 23.4 %all_to_all.11 = f32[16,6,127]{2,1,0:T(8,128)S(1)} all-to-all(f32[16,6,127]{2,1,0:T(8,128)S(1)} %broadcast_in_dim.17), channel_id=1, replica_groups=mesh['cells'=32,'vocab'=16] {'vocab'}, dimensions={0} | all-to-all | bytes 97536 | tf_op jit(solution)/shard_map/all_to_all | solution.py:9
  131.0 0.2 fusion.7
  131.1 0.2 fusion.5
  131.3 0.2 fusion.14
  131.5 0.5 fusion.22
  134.6 0.5 fusion.21
  136.8 1.1 fusion.19
  138.0 1.2 broadcast_in_dim.22
  139.1 7.3 %all-to-all-start.1 = ((f32[32,1,1]{2,1,0:T(1,128)}), f32[32,1,1]{2,1,0:T(1,128)S(1)}, u32[]{:S(2)}, u32[]{:S(2)}) async-start(f32[32,1,1]{2,1,0:T(1,128)} %broadcast_in_dim.22), calls=%async_computation.1 | async-start | bytes 32768 | tf_op jit(solution)/shard_map/all_to_all | solution.py:9
  146.5 0.5 fusion.13
  147.0 6.4 %all-to-all-done.1 = f32[32,1,1]{2,1,0:T(1,128)S(1)} async-done(((f32[32,1,1]{2,1,0:T(1,128)}), f32[32,1,1]{2,1,0:T(1,128)S(1)}, u32[]{:S(2)}, u32[]{:S(2)}) %all-to-all-start.1) | async-done | bytes 160 | tf_op jit(solution)/shard_map/all_to_all | solution.py:9
  153.4 0.6 reduce_sum.91
  (37 shorter events, 0.7 us)
Async XLA Ops:
  7.2 4.1 %copy-start = (bf16[1,4,16,2048]{3,2,1,0:T(8,128)(2,1)S(1)}, bf16[1,4,16,2048]{3,2,1,0:T(8,128)(2,1)}, u32[]{:S(2)}) copy-start(bf16[1,4,16,2048]{3,2,1,0:T(8,128)(2,1)} %param.8) | copy-start | bytes 786436
  7.2 5.3 %copy-start.1 = (f32[1,2048]{1,0:T(1,128)S(1)}, f32[1,2048]{1,0:T(1,128)}, u32[]{:S(2)}) copy-start(f32[1,2048]{1,0:T(1,128)} %param.7) | copy-start | bytes 24580
  7.2 5.3 %copy-start.2 = (f32[2048]{0:T(1024)S(1)}, f32[2048]{0:T(1024)}, u32[]{:S(2)}) copy-start(f32[2048]{0:T(1024)} %param.12) | copy-start | bytes 24580
  7.2 89.0 %all-gather.2.cloned.1.call-start = ((), (), s32[]{:S(2)}) async-start(), calls=%async_computation.2 | async-start | bytes 13516800 | tf_op jit(solution)/shard_map/all_gather | solution.py:120
  139.1 14.3 %all-to-all-start.1 = ((f32[32,1,1]{2,1,0:T(1,128)}), f32[32,1,1]{2,1,0:T(1,128)S(1)}, u32[]{:S(2)}, u32[]{:S(2)}) async-start(f32[32,1,1]{2,1,0:T(1,128)} %broadcast_in_dim.22), calls=%async_computation.1 | async-start | bytes 32768 | tf_op jit(solution)/shard_map/all_to_all | solution.py:9
Sparse Core Ops, SparseCore 0:
  11.1 85.0 all-gather.1
where the time goes:
time: 161 us
  waiting for transfers between devices  90.7 us (56%)
  blocking collectives  23.4 us (15%)
  between operations  19.6 us (12%)
  other arithmetic  8.24 us (5%)
  matrix products  7.84 us (5%)
  starting transfers between devices  7.34 us (5%)
  local copies, waits for them, and re-layouts  3.83 us (2%)
    all_gather x1, waiting for transfers between devices, on_device(): lax.all_gather(unembed, 'cells', axis=0, tiled=True)  83.6 us
    all_to_all x1, blocking collectives, sent_to_all(): lax.all_to_all(jnp.broadcast_to(value[None], (length, *value.shape)), axi...  23.4 us
    all_to_all x1, starting transfers between devices, sent_to_all(): lax.all_to_all(jnp.broadcast_to(value[None], (length, *value.shape)), axi...  7.3 us
    dot_general x1, matrix products, on_device(): jnp.dot(stacked, lax.all_gather(unembed, 'cells', axis=0, tiled=True), pr...  6.69 us
    all_to_all x1, waiting for transfers between devices, sent_to_all(): lax.all_to_all(jnp.broadcast_to(value[None], (length, *value.shape)), axi...  6.42 us
  transfers between devices with their start and end apart: 2, of which 2 were waited for; matrix products, arithmetic and copies ran while one was open for 2% of the time, Pallas kernels for 0%

commit v1 on v0

--- a/solution.py
+++ b/solution.py
@@ -2,6 +2,11 @@
 import jax.numpy as jnp
 from jax import lax
 from jax.sharding import PartitionSpec as P
+
+
+def gather_by_exchange(x, axis, dim):
+    copies = jnp.concatenate([x] * lax.axis_size(axis), axis=dim)
+    return lax.all_to_all(copies, axis, dim, dim, tiled=True)
 
 
 def sent_to_all(value, axis):
@@ -116,9 +121,7 @@
         [normalize_rows(clean_resid, norm_gain), normalize_rows(patched_resid, norm_gain)], axis=0
     )
     logits = jnp.dot(
-        stacked,
-        lax.all_gather(unembed, "cells", axis=0, tiled=True),
-        preferred_element_type=jnp.float32,
+        stacked, gather_by_exchange(unembed, "cells", 0), preferred_element_type=jnp.float32
     )
     columns = vocab_start + jnp.arange(shard_width, dtype=jnp.int32)
     answer_mask = columns[None, :] == answer_ids[:, None]

time: 161 us -> 298 us (1.85)
  waiting for transfers between devices: 90.7 us -> 184 us
  starting transfers between devices: 7.34 us -> 40.1 us
  local copies, waits for them, and re-layouts: 3.83 us -> 25.8 us
  between operations: 19.6 us -> 6.34 us
  blocking collectives: 23.4 us -> 26.8 us
    all_to_all x0 -> x1, waiting for transfers between devices: none -> 178 us  [gather_by_exchange(): return lax.all_to_all(copies, axis, dim, dim, tiled=True)]
    all_gather x1 -> x0, waiting for transfers between devices: 83.6 us -> none  [on_device(): lax.all_gather(unembed, 'cells', axis=0, tiled=True)]
    unnamed x6 -> x45, local copies, waits for them, and re-layouts: 0.02 us -> 22 us
    all_to_all x1, starting transfers between devices: 7.3 us -> 28.5 us  [sent_to_all(): lax.all_to_all(jnp.broadcast_to(value[None], (length, *value.shape)), axi...]
    all_to_all x0 -> x1, starting transfers between devices: none -> 11.6 us  [gather_by_exchange(): return lax.all_to_all(copies, axis, dim, dim, tiled=True)]
    all_to_all x1, blocking collectives: 23.4 us -> 26.8 us  [sent_to_all(): lax.all_to_all(jnp.broadcast_to(value[None], (length, *value.shape)), axi...]
  transfers between devices with their start and end apart: 2 -> 2, of which waited for: 2 -> 2; matrix products, arithmetic and copies ran while one was open for 2% -> 1% of each run, Pallas kernels for 0% -> 0%
where the time goes in v1:
time: 298 us; the launch traced here: 297 us
  waiting for transfers between devices  184 us (62%)
  starting transfers between devices  40.1 us (13%)
  blocking collectives  26.8 us (9%)
  local copies, waits for them, and re-layouts  25.8 us (9%)
  matrix products  7.12 us (2%)
  other arithmetic  6.87 us (2%)
  between operations  6.34 us (2%)
    all_to_all x1, waiting for transfers between devices, gather_by_exchange(): return lax.all_to_all(copies, axis, dim, dim, tiled=True)  178 us
    all_to_all x1, starting transfers between devices, sent_to_all(): lax.all_to_all(jnp.broadcast_to(value[None], (length, *value.shape)), axi...  28.5 us
    all_to_all x1, blocking collectives, sent_to_all(): lax.all_to_all(jnp.broadcast_to(value[None], (length, *value.shape)), axi...  26.8 us
    unnamed x45, local copies, waits for them, and re-layouts  22 us
    all_to_all x1, starting transfers between devices, gather_by_exchange(): return lax.all_to_all(copies, axis, dim, dim, tiled=True)  11.6 us
    dot_general x1, matrix products, on_device(): jnp.dot(stacked, gather_by_exchange(unembed, 'cells', 0), preferred_eleme...  6.69 us
    all_to_all x1, waiting for transfers between devices, sent_to_all(): lax.all_to_all(jnp.broadcast_to(value[None], (length, *value.shape)), axi...  6.46 us
  transfers between devices with their start and end apart: 2, of which 2 were waited for; matrix products, arithmetic and copies ran while one was open for 1% of the time, Pallas kernels for 0%

profile of v1, /device:TPU:1, one launch (start us, length us, event | category | flops | bytes accessed | tf_op | source)
XLA Modules:
  0.0 297.3 jit_solution(8863078326007066246)
XLA Ops:
  0.7 1.1 constant_dynamic-update-slice_fusion.31
  1.8 1.0 constant_dynamic-update-slice_fusion.30
  2.8 1.0 constant_dynamic-update-slice_fusion.29
  3.8 1.0 constant_dynamic-update-slice_fusion.28
  4.9 1.0 constant_dynamic-update-slice_fusion.27
  5.9 1.0 constant_dynamic-update-slice_fusion.26
  7.0 1.0 constant_dynamic-update-slice_fusion.25
  8.0 1.0 constant_dynamic-update-slice_fusion.24
  9.0 1.0 constant_dynamic-update-slice_fusion.23
  10.1 1.0 constant_dynamic-update-slice_fusion.22
  11.1 1.0 constant_dynamic-update-slice_fusion.21
  12.2 1.0 constant_dynamic-update-slice_fusion.20
  13.2 1.0 constant_dynamic-update-slice_fusion.19
  18.1 4.7 %copy-done.2 = bf16[2048,3200]{1,0:T(8,128)(2,1)} copy-done((bf16[2048,3200]{1,0:T(8,128)(2,1)}, bf16[2048,3200]{1,0:T(8,128)(2,1)S(1)}, u32[]{:S(2)}) %copy-start.2) | copy-done | bytes 13107224
  22.8 11.6 %all-to-all-start = ((bf16[32,64,3200]{2,1,0:T(8,128)(2,1)}), bf16[32,64,3200]{2,1,0:T(8,128)(2,1)}, u32[]{:S(2)}, u32[]{:S(2)}) async-start(bf16[32,64,3200]{2,1,0:T(8,128)(2,1)} %bitcast.33), calls=%async_computation | async-start | bytes 26214400 | tf_op jit(solution)/shard_map/all_to_all | solution.py:9
  37.1 177.8 %all-to-all-done = bf16[32,64,3200]{2,1,0:T(8,128)(2,1)} async-done(((bf16[32,64,3200]{2,1,0:T(8,128)(2,1)}), bf16[32,64,3200]{2,1,0:T(8,128)(2,1)}, u32[]{:S(2)}, u32[]{:S(2)}) %all-to-all-start) | async-done | bytes 13107232 | tf_op jit(solution)/shard_map/all_to_all | solution.py:9
  214.9 6.7 %fusion = f32[128,3200]{1,0:T(8,128)S(1)} fusion(bf16[2048,3200]{1,0:T(8,128)(2,1)} %bitcast.4, bf16[127,2048]{1,0:T(8,128)(2,1)S(1)} %multiply_convert_fusion, bf16[1,2048]{1,0:T(2,128)(2,1)S(1)} %multiply_convert_fusion.1), kind=kOutput, calls=%fused_computation.7 | convolution fusion | flops 1678770176 | bytes 15269888 | tf_op jit(solution)/shard_map/dot_general | solution.py:123
  222.2 1.3 fusion.17
  224.5 1.3 pad_bitcast_fusion
  225.9 26.8 %all_to_all.23 = f32[16,6,127]{2,1,0:T(8,128)S(1)} all-to-all(f32[16,6,127]{2,1,0:T(8,128)S(1)} %broadcast_in_dim.17), channel_id=1, replica_groups=mesh['cells'=32,'vocab'=16] {'vocab'}, dimensions={0} | all-to-all | bytes 97536 | tf_op jit(solution)/shard_map/all_to_all | solution.py:14
  258.9 1.1 fusion.19
  260.0 1.2 broadcast_in_dim.22
  261.2 28.5 %all-to-all-start.2 = ((f32[32,1,1]{2,1,0:T(1,128)}), f32[32,1,1]{2,1,0:T(1,128)S(1)}, u32[]{:S(2)}, u32[]{:S(2)}) async-start(f32[32,1,1]{2,1,0:T(1,128)} %broadcast_in_dim.22), calls=%async_computation.2 | async-start | bytes 32768 | tf_op jit(solution)/shard_map/all_to_all | solution.py:14
  290.2 6.5 %all-to-all-done.2 = f32[32,1,1]{2,1,0:T(1,128)S(1)} async-done(((f32[32,1,1]{2,1,0:T(1,128)}), f32[32,1,1]{2,1,0:T(1,128)S(1)}, u32[]{:S(2)}, u32[]{:S(2)}) %all-to-all-start.2) | async-done | bytes 160 | tf_op jit(solution)/shard_map/all_to_all | solution.py:14
  (76 shorter events, 10.0 us)
Async XLA Ops:
  0.6 35.8 %copy-start = (bf16[1,4,16,2048]{3,2,1,0:T(8,128)(2,1)S(1)}, bf16[1,4,16,2048]{3,2,1,0:T(8,128)(2,1)}, u32[]{:S(2)}) copy-start(bf16[1,4,16,2048]{3,2,1,0:T(8,128)(2,1)} %param.8) | copy-start | bytes 786436
  0.6 16.7 %copy-start.1 = (bf16[64,3200]{1,0:T(8,128)(2,1)S(1)}, bf16[64,3200]{1,0:T(8,128)(2,1)}, u32[]{:S(2)}) copy-start(bf16[64,3200]{1,0:T(8,128)(2,1)} %param.13) | copy-start | bytes 1228804
  18.0 4.7 %copy-start.2 = (bf16[2048,3200]{1,0:T(8,128)(2,1)}, bf16[2048,3200]{1,0:T(8,128)(2,1)S(1)}, u32[]{:S(2)}) copy-start(bf16[2048,3200]{1,0:T(8,128)(2,1)S(1)} %constant_dynamic-update-slice_fusion) | copy-start | bytes 39321604
  22.8 11.6 %copy-start.3 = (f32[1,2048]{1,0:T(1,128)S(1)}, f32[1,2048]{1,0:T(1,128)}, u32[]{:S(2)}) copy-start(f32[1,2048]{1,0:T(1,128)} %param.7) | copy-start | bytes 24580
  22.8 13.6 %copy-start.5 = (s32[127]{0:T(128)S(1)}, s32[127]{0:T(128)}, u32[]{:S(2)}) copy-start(s32[127]{0:T(128)} %param.10) | copy-start | bytes 1528
  22.8 13.6 %copy-start.6 = (s32[127]{0:T(128)S(1)}, s32[127]{0:T(128)}, u32[]{:S(2)}) copy-start(s32[127]{0:T(128)} %param.9) | copy-start | bytes 1528
  22.8 14.1 %copy-start.4 = (f32[2048]{0:T(1024)S(1)}, f32[2048]{0:T(1024)}, u32[]{:S(2)}) copy-start(f32[2048]{0:T(1024)} %param.12) | copy-start | bytes 24580
  22.8 192.1 %all-to-all-start = ((bf16[32,64,3200]{2,1,0:T(8,128)(2,1)}), bf16[32,64,3200]{2,1,0:T(8,128)(2,1)}, u32[]{:S(2)}, u32[]{:S(2)}) async-start(bf16[32,64,3200]{2,1,0:T(8,128)(2,1)} %bitcast.33), calls=%async_computation | async-start | bytes 26214400 | tf_op jit(solution)/shard_map/all_to_all | solution.py:9
  261.2 35.5 %all-to-all-start.2 = ((f32[32,1,1]{2,1,0:T(1,128)}), f32[32,1,1]{2,1,0:T(1,128)S(1)}, u32[]{:S(2)}, u32[]{:S(2)}) async-start(f32[32,1,1]{2,1,0:T(1,128)} %broadcast_in_dim.22), calls=%async_computation.2 | async-start | bytes 32768 | tf_op jit(solution)/shard_map/all_to_all | solution.py:14
